TPU v7x, 32 devices: a whole 2x2x4 slice. The times are simulated.
32 devices in a mesh: energy: 16 (over z, x, core), seg: 2 (over y).
Axes of the slice: x: 2, y: 2, z: 4, core: 2. Of those that a mesh axis runs over, the one named last changes fastest.
Arguments:
- onsite: float32 [2, 384, 384], P('seg'), may hold values from -3 to 8
- coupling: float32 [2, 384, 384], P('seg'), may hold values from -2 to 2
- phonon: float32 [2, 384, 384], P('seg'), may hold values from -1 to 1
- levels: float32 [16], P('energy'), may hold values from 0.5 to 2
- offsets: int32 [2], replicated, may hold values from 1 to 15
Outputs:
- green_fn: float32 [16, 2, 384, 384], P('energy', 'seg')
- self_energy: float32 [16, 2, 384, 384], P('energy', 'seg')
All inputs are finite; a program needn't handle non-finite values.
Results may differ from a plain program's by a relative error of at most 0.0001.
Values sent between devices are 32-bit elements; how exact they have to be, the bound alone decides.
No kernel may reach another device: no remote copies, remote signals or barrier semaphores. Data moves between devices by JAX's collectives and lax.ppermute only.
A program may use at most 64 MiB of HBM per device.

v0:
```python
import functools
import math

import jax
import jax.numpy as jnp
from jax import lax
from jax.experimental import pallas as pl
from jax.experimental.pallas import tpu as pltpu
from jax.sharding import PartitionSpec as P


NS = 4
TERMS = 4
VMEM_BYTES = 52 * 2**20
SPARE_BYTES = 8 * 2**20
F32, BF16 = jnp.float32, jnp.bfloat16


def split(x):
    high = x.astype(BF16)
    return high, (x - high.astype(F32)).astype(BF16)


def product(a, b):
    left = jnp.concatenate([a[0], a[0], a[1]], axis=1)
    right = jnp.concatenate([b[0], b[1], b[0]], axis=0)
    return jnp.dot(left, right, preferred_element_type=F32)


def beside(a, b):
    return tuple(jnp.concatenate([x, y], axis=1) for x, y in zip(a, b))


def joined(a):
    return a[0].astype(F32) + a[1].astype(F32)


def eye_mask(n):
    return lax.broadcasted_iota(jnp.int32, (n, n), 0) == lax.broadcasted_iota(jnp.int32, (n, n), 1)


def diagonal(x, axis):
    n, step = x.shape[0], 128
    mask = eye_mask(step)
    blocks = [
        jnp.sum(jnp.where(mask, x[i : i + step, i : i + step], 0.0), axis=axis, keepdims=True)
        for i in range(0, n, step)
    ]
    return jnp.concatenate(blocks, axis=1 - axis)


def over(low, high, body):
    if high - low == 1:
        body(low)
    elif high > low:
        lax.fori_loop(low, high, lambda s, _: (body(s), None)[1], None)


class Pair:
    def __init__(self, ref):
        self.ref = ref

    def put(self, index, value):
        self.ref[(*index, 0)], self.ref[(*index, 1)] = split(value)

    def get(self, *index):
        return self.ref[(*index, 0)], self.ref[(*index, 1)]


def invert(matrices, power, poly, row_scale, store):
    lanes = range(len(matrices))
    for i in lanes:
        x = matrices[i]()
        n = x.shape[0]
        identity = jnp.where(eye_mask(n), 1.0, 0.0)
        residual = identity - x * (1.0 / diagonal(x, 0))
        row_scale[i] = jnp.broadcast_to(1.0 / diagonal(x, 1), (n, 128))
        power.put((i,), residual)
        poly.put((i,), identity + residual)
    for i in lanes:
        e = power.get(i)
        power.put((i,), product(e, e))
    for _ in range(2, NS):
        for i in lanes:
            e, p = power.get(i), poly.get(i)
            both = product(e, beside(e, p))
            n = both.shape[0]
            power.put((i,), both[:, :n])
            poly.put((i,), both[:, n:] + joined(p))
    for i in lanes:
        p = poly.get(i)
        total = product(power.get(i), p) + joined(p)
        n = total.shape[0]
        store(i, total * jnp.concatenate([row_scale[i]] * (n // 128), axis=1))


def sweep(lanes, segs, matrix, coupling, coupling_t, left, left_pair, green, work, power, poly, row_scale, emit, wanted=None, given=False):
    right, outer = work

    def forward(s):
        def load(i):
            x = matrix(s, i)
            if not (isinstance(s, int) and s == 0):
                x = x - left[s, i]
            return x

        def store(i, value):
            left[s, i] = value
            left_pair.put((i,), value)

        invert([functools.partial(load, i) for i in range(lanes)], power, poly, row_scale, store)

    def hand_over(s):
        for i in range(lanes):
            outer.put((s, i), product(left_pair.get(i), coupling_t.get(s + 1)))
        for i in range(lanes):
            both = product(coupling.get(s + 1), beside(left_pair.get(i), outer.get(s, i)))
            n = both.shape[0]
            right.put((s, i), both[:, :n])
            left[s + 1, i] = both[:, n:]

    if given:
        for i in range(lanes):
            left_pair.put((i,), left[0, i])
    else:
        forward(0)

    def advance(s):
        hand_over(s - 1)
        forward(s)

    over(1, segs, advance)
    for i in range(lanes):
        green.put((i,), left[segs - 1, i])
        emit(segs - 1, i, left[segs - 1, i])

    def backward(turn):
        s = segs - 1 - turn

        def settle():
            for i in range(lanes):
                green.put((i,), product(green.get(i), right.get(s, i)))
            for i in range(lanes):
                value = left[s, i] + product(outer.get(s, i), green.get(i))
                green.put((i,), value)
                emit(s, i, value)

        if wanted is None:
            settle()
        else:
            pl.when(wanted(s))(settle)

    over(1, segs, backward)


def pieces(target, own, received, at):
    seg, segs, parity = at
    copies = [(own, target.at[seg])]
    for d in range(1, segs):
        source = lax.rem(seg - d + segs, segs)
        copies += parts(received[d - 1], target.at[source], parity)
    return copies


def parts(received, target, parity):
    if len(received) == 1:
        return [(received[0], target)]
    half = target.shape[0] // 2
    return [
        (block, target.at[pl.ds(pl.multiple_of(which * half, half), half), :])
        for block, which in zip(received, (parity, 1 - parity))
    ]


def started(ends, sems):
    copies = [pltpu.make_async_copy(*pair, sems.at[k]) for k, pair in enumerate(ends)]
    for copy in copies:
        copy.start()
    return copies


def wait(copies):
    for copy in copies:
        copy.wait()


def taken(refs, segs, each):
    own, *refs = refs
    return own, [refs[each * k : each * (k + 1)] for k in range(segs - 1)], refs[each * (segs - 1) :]


def choose(index, levels, chosen, count):
    total = jnp.int32(0)
    for sign in (-1, 1):
        for k in range(2):
            source = index[0] + sign * index[2 + k]
            inside = (source >= 0) & (source < count)
            chosen[total] = levels[jnp.clip(source, 0, count - 1)]
            total = total + inside.astype(jnp.int32)
    return total


def in_turns(total, lanes, turn):
    whole = total // lanes
    lax.fori_loop(0, whole, lambda k, _: (turn(k * lanes, lanes), None)[1], None)
    if lanes > 1:
        lax.fori_loop(whole * lanes, total, lambda k, _: (turn(k, 1), None)[1], None)


def first_blocks(segs, count, lanes, index, levels, *refs):
    own, received, (left, onsite, power, poly, row_scale, sems, chosen) = taken(refs, segs, 2)
    seg, parity = index[1], lax.rem(index[0], 2)
    n = onsite.shape[0]

    @pl.when(seg == 0)
    def _():
        wait(started([(own, onsite)], sems))

    for d in range(1, segs):

        @pl.when(seg == d)
        def _():
            wait(started(parts(received[d - 1], onsite, parity), sems))

    total = choose(index, levels, chosen, count)

    def turn(at, width):
        def load(i):
            return onsite[...] + jnp.where(eye_mask(n), chosen[at + i], 0.0)

        def store(i, value):
            left[at + i] = value

        invert([functools.partial(load, i) for i in range(width)], Pair(power), Pair(poly), row_scale, store)

    in_turns(total, lanes, turn)


def prepared(stage, coupling, coupling_t, segs):
    def prepare(s):
        value = stage[s]
        coupling.put((s,), value)
        coupling_t.put((s,), value.T)

    over(1, segs, prepare)


def first_round(segs, count, lanes, index, levels, *refs):
    own_matrix, received_matrix, refs = taken(refs, segs, 2)
    own_coupling, received_coupling, refs = taken(refs, segs, 1)
    first, combined, onsite, coupling, coupling_t, stage, left, left_pair, green, right, outer, power, poly, row_scale, sems, chosen, firsts = refs
    at = (index[1], segs, lax.rem(index[0], 2))
    copies = started(pieces(stage, own_coupling, received_coupling, at), sems.at[0])
    copies += started([(first, firsts)], sems.at[2])
    later = started(pieces(onsite, own_matrix, received_matrix, at), sems.at[1])
    total = choose(index, levels, chosen, count)
    combined[...] = jnp.zeros_like(combined)
    wait(copies)
    coupling, coupling_t = Pair(coupling), Pair(coupling_t)
    prepared(stage, coupling, coupling_t, segs)
    wait(later)
    n = onsite.shape[1]

    def turn(at, width):
        for i in range(width):
            left[0, i] = firsts[at + i]

        def matrix(s, i):
            return onsite[s] + jnp.where(eye_mask(n), chosen[at + i], 0.0)

        def emit(s, i, value):
            combined[s] += value

        sweep(
            width, segs, matrix, coupling, coupling_t, left, Pair(left_pair), Pair(green),
            (Pair(right), Pair(outer)), Pair(power), Pair(poly), row_scale, emit, given=True,
        )

    in_turns(total, lanes, turn)


def second_round(segs, index, level, *refs):
    own_matrix, received_matrix, refs = taken(refs, segs, 2)
    own_coupling, received_coupling, refs = taken(refs, segs, 1)
    own_phonon, received_phonon, refs = taken(refs, segs, 1)
    combined_in, green_out, energy_out, *refs = refs
    onsite, coupling, coupling_t, stage, left, left_pair, green, right, outer, power, poly, row_scale, sems, phonon, combined = refs
    seg = index[1]
    at = (seg, segs, lax.rem(index[0], 2))
    copies = started([(combined_in, combined)], sems.at[3])
    copies += started(pieces(phonon, own_phonon, received_phonon, at), sems.at[2])
    later = started(pieces(onsite, own_matrix, received_matrix, at), sems.at[0])
    later += started(pieces(stage, own_coupling, received_coupling, at), sems.at[1])
    coupling, coupling_t, right, outer = Pair(coupling), Pair(coupling_t), Pair(right), Pair(outer)
    n = onsite.shape[1]
    wait(copies)
    for s in range(segs):
        value = phonon[s]
        coupling.put((s,), value)
        coupling_t.put((s,), value.T)
        right.put((s, 0), combined[s])
    for s in range(segs):
        outer.put((s, 0), product(coupling.get(s), right.get(s, 0)))
    for s in range(segs):
        combined[s] = product(outer.get(s, 0), coupling_t.get(s))
    energy_out[...] = combined[seg]
    wait(later)

    def matrix(s, i):
        return onsite[s] + jnp.where(eye_mask(n), level[0], 0.0) + combined[s]

    def emit(s, i, value):
        @pl.when(seg == s)
        def _():
            green_out[...] = value

    prepared(stage, coupling, coupling_t, segs)
    sweep(
        1, segs, matrix, coupling, coupling_t, left, Pair(left_pair), Pair(green),
        (right, outer), Pair(power), Pair(poly), row_scale, emit, lambda s: seg <= s,
    )


def pair(n, *lead):
    return pltpu.VMEM((*lead, 2, n, n), BF16)


def full(n, *lead):
    return pltpu.VMEM((*lead, n, n), F32)


def workspace(segs, n, lanes):
    return [
        full(n, segs), pair(n, segs), pair(n, segs), full(n, segs), full(n, segs, lanes), pair(n, lanes), pair(n, lanes),
        pair(n, segs, lanes), pair(n, segs, lanes), pair(n, lanes), pair(n, lanes), pltpu.VMEM((lanes, n, 128), F32),
        pltpu.SemaphoreType.DMA((4, 2 * segs)),
    ]


def held(shapes):
    return sum(4 * math.prod(s.shape) for s in shapes if s.dtype == F32) + sum(2 * math.prod(s.shape) for s in shapes if s.dtype == BF16)


def call(body, out_shape, operands, scratch, flops):
    smem, vmem, anywhere = (pl.BlockSpec(memory_space=m) for m in (pltpu.SMEM, pltpu.VMEM, pl.ANY))
    outs = jax.tree.leaves(out_shape)
    return pl.pallas_call(
        body,
        out_shape=out_shape,
        in_specs=[smem, smem] + [anywhere] * (len(operands) - 2),
        out_specs=jax.tree.map(lambda _: vmem, out_shape),
        scratch_shapes=scratch,
        compiler_params=pltpu.CompilerParams(vmem_limit_bytes=held(scratch + outs) + SPARE_BYTES),
        cost_estimate=pl.CostEstimate(flops=flops, bytes_accessed=held(outs), transcendentals=0),
    )(*operands)


def swapped(block, axis, distance):
    size = lax.axis_size(axis)
    return lax.ppermute(block, axis, [(i, (i + distance) % size) for i in range(size)])


def partner(block, axis, bit):
    size = lax.axis_size(axis)
    return lax.ppermute(block, axis, [(i, i ^ bit) for i in range(size)])


def every_level(levels):
    size, bit = lax.axis_size("energy"), 1
    place_of = lax.axis_index("energy")
    while bit < size:
        other = partner(levels, "energy", bit)
        low = place_of & bit == 0
        levels = jnp.where(low, jnp.concatenate([levels, other]), jnp.concatenate([other, levels]))
        bit *= 2
    return levels


def half_of(block):
    half = block.shape[0] // 2
    return lax.dynamic_slice_in_dim(block, lax.axis_index("energy") % 2 * half, half, 0)


def from_others(block):
    received = []
    for d in range(1, lax.axis_size("seg")):
        received.append(swapped(block, "seg", d))
    return received


def with_partner(halves):
    return [part for half in halves for part in (half, partner(half, "energy", 1))]


def shards(onsite, coupling, phonon, levels, offsets):
    return both_rounds(onsite[0], coupling[0], phonon[0], levels, offsets)


def both_rounds(onsite, coupling, phonon, levels, offsets):
    segs, count = lax.axis_size("seg"), lax.axis_size("energy")
    n = onsite.shape[-1]
    energy, seg = lax.axis_index("energy"), lax.axis_index("seg")

    def less_lead(block, rows):
        lead = jnp.matmul(rows, coupling.T, precision=lax.Precision.HIGH) * 0.25
        return block - jnp.where(seg == 0, lead, 0.0)

    matrix_half = less_lead(half_of(onsite), half_of(coupling))
    halves = from_others(matrix_half)
    matrices = with_partner(halves)
    all_levels = every_level(levels)
    matrix = less_lead(onsite, lax.optimization_barrier((coupling, matrix_half))[0])
    couplings = from_others(coupling)
    phonons = from_others(phonon)
    index = jnp.concatenate([jnp.stack([energy, seg]).astype(jnp.int32), offsets])
    lanes = 2 if held(workspace(segs, n, 2)) + segs * 4 * n * n < VMEM_BYTES else 1
    shape = functools.partial(jax.ShapeDtypeStruct, dtype=F32)
    chosen = pltpu.SMEM((2 * TERMS,), jnp.float32)
    first = call(
        functools.partial(first_blocks, segs, count, lanes),
        shape((TERMS, n, n)),
        [index, all_levels, matrix, *matrices],
        [full(n), pair(n, lanes), pair(n, lanes), pltpu.VMEM((lanes, n, 128), F32), pltpu.SemaphoreType.DMA((2,)), chosen],
        12 * n**3 * TERMS * 3,
    )
    combined = call(
        functools.partial(first_round, segs, count, lanes),
        shape((segs, n, n)),
        [index, all_levels, matrix, *matrices, coupling, *couplings, first],
        workspace(segs, n, lanes) + [chosen, full(n, TERMS)],
        22 * n**3 * TERMS * 3 * (segs - 1),
    )
    green, self_energy = call(
        functools.partial(second_round, segs),
        [shape((n, n))] * 2,
        [index, levels, matrix, *matrices, coupling, *couplings, phonon, *phonons, combined],
        workspace(segs, n, 1) + [full(n, segs), full(n, segs)],
        36 * n**3 * 3,
    )
    return green[None, None], self_energy[None, None]


def solution(mesh):
    in_specs = (P("seg", None, None), P("seg", None, None), P("seg", None, None), P("energy"), P())
    out_specs = (P("energy", "seg", None, None), P("energy", "seg", None, None))
    return jax.shard_map(shards, mesh=mesh, in_specs=in_specs, out_specs=out_specs, check_vma=False)
```

profile of v0, /device:TPU:0, one launch (start us, length us, event | category | flops | bytes accessed | tf_op | source)
XLA Modules:
  0.0 56.0 jit_solution(9710679595112117492)
XLA Ops:
  0.6 0.0 copy-start.2
  0.7 1.7 %fusion.3 = f32[192,384]{1,0:T(8,128)S(1)} fusion(f32[1,384,384]{2,1,0:T(8,128)} %param.6, s32[]{:T(128)S(6)} %select_n.63, f32[1,384,384]{2,1,0:T(8,128)} %param.5, pred[]{:T(512)S(6)} %eq.19), kind=kOutput, calls=%fused_computation.5 | convolution fusion | flops 170090496 | bytes 1476096 | tf_op jit(solution)/shard_map/dot_general | solution.py:405
  2.4 3.1 %collective-permute-start = (f32[192,384]{1,0:T(8,128)S(1)}, f32[192,384]{1,0:T(8,128)S(1)}, u32[]{:S(2)}, u32[]{:S(2)}) collective-permute-start(f32[192,384]{1,0:T(8,128)S(1)} %fusion.3), channel_id=1, source_target_pairs={{0,1},{1,0},{2,3},{3,2},{4,5},{5,4},{6,7},{7,6},{8,9},{9,8},{10,11... | collective-permute-start | bytes 884744 | tf_op jit(solution)/shard_map/ppermute | solution.py:360
  5.4 0.0 collective-permute-start.4
  5.4 0.2 collective-permute-start.2
  5.6 1.9 %collective-permute-start.3 = (f32[384,384]{1,0:T(8,128)}, f32[384,384]{1,0:T(8,128)S(1)}, u32[]{:S(2)}, u32[]{:S(2)}) collective-permute-start(f32[384,384]{1,0:T(8,128)} %bitcast.22), channel_id=1, source_target_pairs={{0,1},{1,0},{2,3},{3,2},{4,5},{5,4},{6,7},{7,6},{8,9},{9,8},{10,11... | collective-permute-start | bytes 1769480 | tf_op jit(solution)/shard_map/ppermute | solution.py:360
  7.5 2.1 %fusion.1.refs_0_ = f32[384,384]{1,0:T(8,128)S(1)} fusion(f32[384,384]{1,0:T(8,128)} %bitcast.19, f32[1,384,384]{2,1,0:T(8,128)} %param.5, pred[]{:T(512)S(6)} %eq.19, f32[1,384,384]{2,1,0:T(8,128)} %param.6), kind=kOutput, calls=%fused_computation.2 | convolution fusion | flops 340180992 | bytes 2359297 | tf_op jit(solution)/shard_map/dot_general | solution.py:405
  10.3 0.0 copy-done.2
  10.3 0.1 pad_add_fusion.index
  10.4 0.0 collective-permute-done.4
  10.4 0.7 %broadcast_select_fusion = f32[2]{0:T(128)S(1)} fusion(pred[]{:T(512)S(6)} %eq.23, f32[1]{0:T(128)} %collective-permute-done.4, f32[1]{0:T(128)S(6)} %copy.7.level), kind=kLoop, calls=%fused_computation.8 | loop fusion | flops 6 | bytes 17 | tf_op jit(solution)/shard_map/jit(_where)/select_n | solution.py:374
  11.1 1.5 %collective-permute-start.5 = (f32[2]{0:T(128)S(1)}, f32[2]{0:T(128)S(1)}, u32[]{:S(2)}, u32[]{:S(2)}) collective-permute-start(f32[2]{0:T(128)S(1)} %broadcast_select_fusion), channel_id=1, source_target_pairs={{0,4},{2,6},{4,0},{6,2},{8,12},{10,14},{12,8},{14,10},{16,20},{18,... | collective-permute-start | bytes 32 | tf_op jit(solution)/shard_map/ppermute | solution.py:365
  12.6 0.7 %collective-permute-done.refs_1_ = f32[192,384]{1,0:T(8,128)S(1)} collective-permute-done((f32[192,384]{1,0:T(8,128)S(1)}, f32[192,384]{1,0:T(8,128)S(1)}, u32[]{:S(2)}, u32[]{:S(2)}) %collective-permute-start) | collective-permute-done | bytes 294944 | tf_op jit(solution)/shard_map/ppermute | solution.py:360
  13.3 0.0 collective-permute-start.1
  13.3 1.3 %collective-permute-done.5 = f32[2]{0:T(128)S(1)} collective-permute-done((f32[2]{0:T(128)S(1)}, f32[2]{0:T(128)S(1)}, u32[]{:S(2)}, u32[]{:S(2)}) %collective-permute-start.5) | collective-permute-done | bytes 40 | tf_op jit(solution)/shard_map/ppermute | solution.py:365
  14.6 0.1 broadcast_select_fusion.1
  14.7 1.6 %collective-permute-start.6 = (f32[4]{0:T(128)S(1)}, f32[4]{0:T(128)S(1)}, u32[]{:S(2)}, u32[]{:S(2)}) collective-permute-start(f32[4]{0:T(128)S(1)} %broadcast_select_fusion.1), channel_id=1, source_target_pairs={{0,8},{2,10},{4,12},{6,14},{8,0},{10,2},{12,4},{14,6},{16,24},{18,... | collective-permute-start | bytes 56 | tf_op jit(solution)/shard_map/ppermute | solution.py:365
  16.3 2.0 %collective-permute-done.6 = f32[4]{0:T(128)S(1)} collective-permute-done((f32[4]{0:T(128)S(1)}, f32[4]{0:T(128)S(1)}, u32[]{:S(2)}, u32[]{:S(2)}) %collective-permute-start.6) | collective-permute-done | bytes 48 | tf_op jit(solution)/shard_map/ppermute | solution.py:365
  18.3 0.1 broadcast_select_fusion.2
  18.4 2.6 %collective-permute-start.7 = (f32[8]{0:T(128)S(1)}, f32[8]{0:T(128)S(1)}, u32[]{:S(2)}, u32[]{:S(2)}) collective-permute-start(f32[8]{0:T(128)S(1)} %broadcast_select_fusion.2), channel_id=1, source_target_pairs={{0,16},{2,18},{4,20},{6,22},{8,24},{10,26},{12,28},{14,30},{16,0},... | collective-permute-start | bytes 104 | tf_op jit(solution)/shard_map/ppermute | solution.py:365
  21.0 1.9 %collective-permute-done.7 = f32[8]{0:T(128)S(1)} collective-permute-done((f32[8]{0:T(128)S(1)}, f32[8]{0:T(128)S(1)}, u32[]{:S(2)}, u32[]{:S(2)}) %collective-permute-start.7) | collective-permute-done | bytes 64 | tf_op jit(solution)/shard_map/ppermute | solution.py:365
  22.8 0.1 broadcast_select_fusion.3.levels
  22.9 0.0 copy-start
  22.9 0.0 collective-permute-done.1.refs_2_
  22.9 6.2 %shard_map.68.refs_5_ = f32[4,384,384]{2,1,0:T(8,128)S(1)} custom-call(s32[4]{0:T(128)S(1)} %pad_add_fusion.index, f32[16]{0:T(128)S(1)} %broadcast_select_fusion.3.levels, f32[384,384]{1,0:T(8,128)S(1)} %fusion.1.refs_0_, f32[192,384]{1,0:T(8,128)S(1)} %collective-permute-done.refs_1_, f32[192,384]{1,0:T(8,128)S(1)} %collective-permute-done.1.refs_2_), custom_call_target="tpu_custom_call" | custom-call | flops 8153726976 | bytes 2359296 | tf_op jit(solution)/shard_map/pallas_call | solution.py:347
  29.2 0.0 copy-start.1
  29.2 0.0 collective-permute-done.2.refs_4_
  29.2 0.0 copy-done
  29.2 12.2 %shard_map.69.refs_7_ = f32[2,384,384]{2,1,0:T(8,128)S(1)} custom-call(s32[4]{0:T(128)S(1)} %pad_add_fusion.index, f32[16]{0:T(128)S(1)} %broadcast_select_fusion.3.levels, f32[384,384]{1,0:T(8,128)S(1)} %fusion.1.refs_0_, f32[192,384]{1,0:T(8,128)S(1)} %collective-permute-done.refs_1_, f32[192,384]{1,0:T(8,128)S(1)} %collective-permute-done.1.refs_2_, ...), custom_call_target="tpu_custom_call" | custom-call | flops 14948499456 | bytes 1179648 | tf_op jit(solution)/shard_map/pallas_call | solution.py:347
  41.4 0.0 collective-permute-done.3.refs_6_
  41.4 0.0 copy-done.1
  41.4 14.4 %shard_map.70 = (f32[384,384]{1,0:T(8,128)}, f32[384,384]{1,0:T(8,128)}) custom-call(s32[4]{0:T(128)S(1)} %pad_add_fusion.index, f32[1]{0:T(128)S(6)} %copy.7.level, f32[384,384]{1,0:T(8,128)S(1)} %fusion.1.refs_0_, f32[192,384]{1,0:T(8,128)S(1)} %collective-permute-done.refs_1_, f32[192,384]{1,0:T(8,128)S(1)} %collective-permute-done.1.refs_2_, ...), custom_call_target="tpu_custom_call" | custom-call | flops 6115295232 | bytes 1179648 | tf_op jit(solution)/shard_map/pallas_call | solution.py:347
Async XLA Ops:
  0.6 9.6 %copy-start.2 = (s32[2]{0:T(128)S(1)}, s32[2]{0:T(128)}, u32[]{:S(2)}) copy-start(s32[2]{0:T(128)} %param.9) | copy-start | bytes 28
  2.4 10.9 %collective-permute-start = (f32[192,384]{1,0:T(8,128)S(1)}, f32[192,384]{1,0:T(8,128)S(1)}, u32[]{:S(2)}, u32[]{:S(2)}) collective-permute-start(f32[192,384]{1,0:T(8,128)S(1)} %fusion.3), channel_id=1, source_target_pairs={{0,1},{1,0},{2,3},{3,2},{4,5},{5,4},{6,7},{7,6},{8,9},{9,8},{10,11... | collective-permute-start | bytes 884744 | tf_op jit(solution)/shard_map/ppermute | solution.py:360
  5.4 4.9 %collective-permute-start.4 = (f32[1]{0:T(128)}, f32[1]{0:T(128)}, u32[]{:S(2)}, u32[]{:S(2)}) collective-permute-start(f32[1]{0:T(128)} %param.8), channel_id=1, source_target_pairs={{0,2},{2,0},{4,6},{6,4},{8,10},{10,8},{12,14},{14,12},{16,18},{18,... | collective-permute-start | bytes 20 | tf_op jit(solution)/shard_map/ppermute | solution.py:365
  5.4 23.7 %collective-permute-start.2 = (f32[384,384]{1,0:T(8,128)}, f32[384,384]{1,0:T(8,128)S(1)}, u32[]{:S(2)}, u32[]{:S(2)}) collective-permute-start(f32[384,384]{1,0:T(8,128)} %bitcast.18), channel_id=1, source_target_pairs={{0,1},{1,0},{2,3},{3,2},{4,5},{5,4},{6,7},{7,6},{8,9},{9,8},{10,11... | collective-permute-start | bytes 1769480 | tf_op jit(solution)/shard_map/ppermute | solution.py:360
  5.6 35.8 %collective-permute-start.3 = (f32[384,384]{1,0:T(8,128)}, f32[384,384]{1,0:T(8,128)S(1)}, u32[]{:S(2)}, u32[]{:S(2)}) collective-permute-start(f32[384,384]{1,0:T(8,128)} %bitcast.22), channel_id=1, source_target_pairs={{0,1},{1,0},{2,3},{3,2},{4,5},{5,4},{6,7},{7,6},{8,9},{9,8},{10,11... | collective-permute-start | bytes 1769480 | tf_op jit(solution)/shard_map/ppermute | solution.py:360
  11.1 3.6 %collective-permute-start.5 = (f32[2]{0:T(128)S(1)}, f32[2]{0:T(128)S(1)}, u32[]{:S(2)}, u32[]{:S(2)}) collective-permute-start(f32[2]{0:T(128)S(1)} %broadcast_select_fusion), channel_id=1, source_target_pairs={{0,4},{2,6},{4,0},{6,2},{8,12},{10,14},{12,8},{14,10},{16,20},{18,... | collective-permute-start | bytes 32 | tf_op jit(solution)/shard_map/ppermute | solution.py:365
  13.3 9.6 %collective-permute-start.1 = (f32[192,384]{1,0:T(8,128)S(1)}, f32[192,384]{1,0:T(8,128)S(1)}, u32[]{:S(2)}, u32[]{:S(2)}) collective-permute-start(f32[192,384]{1,0:T(8,128)S(1)} %collective-permute-done.refs_1_), channel_id=1, source_target_pairs={{0,2},{2,0},{4,6},{6,4},{8,10},{10,8},{12,14},{14,12},{16,18},{18,... | collective-permute-start | bytes 884744 | tf_op jit(solution)/shard_map/ppermute | solution.py:365
  14.7 3.6 %collective-permute-start.6 = (f32[4]{0:T(128)S(1)}, f32[4]{0:T(128)S(1)}, u32[]{:S(2)}, u32[]{:S(2)}) collective-permute-start(f32[4]{0:T(128)S(1)} %broadcast_select_fusion.1), channel_id=1, source_target_pairs={{0,8},{2,10},{4,12},{6,14},{8,0},{10,2},{12,4},{14,6},{16,24},{18,... | collective-permute-start | bytes 56 | tf_op jit(solution)/shard_map/ppermute | solution.py:365
  18.4 4.5 %collective-permute-start.7 = (f32[8]{0:T(128)S(1)}, f32[8]{0:T(128)S(1)}, u32[]{:S(2)}, u32[]{:S(2)}) collective-permute-start(f32[8]{0:T(128)S(1)} %broadcast_select_fusion.2), channel_id=1, source_target_pairs={{0,16},{2,18},{4,20},{6,22},{8,24},{10,26},{12,28},{14,30},{16,0},... | collective-permute-start | bytes 104 | tf_op jit(solution)/shard_map/ppermute | solution.py:365
  22.9 6.3 %copy-start = (f32[1,384,384]{2,1,0:T(8,128)S(1)}, f32[1,384,384]{2,1,0:T(8,128)}, u32[]{:S(2)}) copy-start(f32[1,384,384]{2,1,0:T(8,128)} %param.6) | copy-start | bytes 1769476
  29.2 12.2 %copy-start.1 = (f32[1,384,384]{2,1,0:T(8,128)S(1)}, f32[1,384,384]{2,1,0:T(8,128)}, u32[]{:S(2)}) copy-start(f32[1,384,384]{2,1,0:T(8,128)} %param.7) | copy-start | bytes 1769476
where the time goes:
time: 56.2 us; the launch traced here: 56 us
  Pallas kernels  32.8 us (58%)
  starting transfers between devices  10.8 us (19%)
  waiting for transfers between devices  5.95 us (11%)
  matrix products  3.85 us (7%)
  between operations  1.59 us (3%)
  other arithmetic  1 us (2%)
    pallas_call x3, Pallas kernels, call(): pl.pallas_call(body, out_shape=out_shape, in_specs=[smem, smem] + [anywhe...  32.8 us
    ppermute x5, starting transfers between devices, partner(): return lax.ppermute(block, axis, [(i, i ^ bit) for i in range(size)])  5.68 us
    ppermute x5, waiting for transfers between devices, partner(): return lax.ppermute(block, axis, [(i, i ^ bit) for i in range(size)])  5.21 us
    ppermute x3, starting transfers between devices, swapped(): lax.ppermute(block, axis, [(i, (i + distance) % size) for i in range(size)])  5.08 us
    dot_general x2, matrix products, less_lead(): lead = jnp.matmul(rows, coupling.T, precision=lax.Precision.HIGH) * 0.25  3.85 us
  transfers between devices with their start and end apart: 8, of which 4 were waited for; matrix products, arithmetic and copies ran while one was open for 6% of the time, Pallas kernels for 33%

commit v1 on v0

--- a/solution.py
+++ b/solution.py
@@ -11,6 +11,7 @@
 
 NS = 4
 TERMS = 4
+TAIL = 128
 VMEM_BYTES = 52 * 2**20
 SPARE_BYTES = 8 * 2**20
 F32, BF16 = jnp.float32, jnp.bfloat16
@@ -21,10 +22,15 @@
     return high, (x - high.astype(F32)).astype(BF16)
 
 
-def product(a, b):
-    left = jnp.concatenate([a[0], a[0], a[1]], axis=1)
-    right = jnp.concatenate([b[0], b[1], b[0]], axis=0)
-    return jnp.dot(left, right, preferred_element_type=F32)
+def product(a, b, alone=False):
+    rows = a[0].shape[0]
+    cut = rows - TAIL if alone else rows
+    order = [(which, lo, hi) for lo, hi in ((0, cut), (cut, rows)) if lo < hi for which in ((0, 0), (0, 1), (1, 0))]
+    left = jnp.concatenate([a[i][:, lo:hi] for (i, _), lo, hi in order], axis=1)
+    right = jnp.concatenate([b[j][lo:hi] for (_, j), lo, hi in order], axis=0)
+    parts = [left[:cut], left[cut:]] if alone else [left]
+    parts = [jnp.dot(part, right, preferred_element_type=F32) for part in parts]
+    return jnp.concatenate(parts, axis=0) if alone else parts[0]
 
 
 def beside(a, b):
@@ -69,6 +75,7 @@
 
 def invert(matrices, power, poly, row_scale, store):
     lanes = range(len(matrices))
+    alone = len(matrices) == 1
     for i in lanes:
         x = matrices[i]()
         n = x.shape[0]
@@ -79,23 +86,24 @@
         poly.put((i,), identity + residual)
     for i in lanes:
         e = power.get(i)
-        power.put((i,), product(e, e))
+        power.put((i,), product(e, e, alone))
     for _ in range(2, NS):
         for i in lanes:
             e, p = power.get(i), poly.get(i)
-            both = product(e, beside(e, p))
+            both = product(e, beside(e, p), alone)
             n = both.shape[0]
             power.put((i,), both[:, :n])
             poly.put((i,), both[:, n:] + joined(p))
     for i in lanes:
         p = poly.get(i)
-        total = product(power.get(i), p) + joined(p)
+        total = product(power.get(i), p, alone) + joined(p)
         n = total.shape[0]
         store(i, total * jnp.concatenate([row_scale[i]] * (n // 128), axis=1))
 
 
 def sweep(lanes, segs, matrix, coupling, coupling_t, left, left_pair, green, work, power, poly, row_scale, emit, wanted=None, given=False):
     right, outer = work
+    alone = lanes == 1
 
     def forward(s):
         def load(i):
@@ -112,9 +120,9 @@
 
     def hand_over(s):
         for i in range(lanes):
-            outer.put((s, i), product(left_pair.get(i), coupling_t.get(s + 1)))
+            outer.put((s, i), product(left_pair.get(i), coupling_t.get(s + 1), alone))
         for i in range(lanes):
-            both = product(coupling.get(s + 1), beside(left_pair.get(i), outer.get(s, i)))
+            both = product(coupling.get(s + 1), beside(left_pair.get(i), outer.get(s, i)), alone)
             n = both.shape[0]
             right.put((s, i), both[:, :n])
             left[s + 1, i] = both[:, n:]
@@ -139,9 +147,9 @@
 
         def settle():
             for i in range(lanes):
-                green.put((i,), product(green.get(i), right.get(s, i)))
+                green.put((i,), product(green.get(i), right.get(s, i), alone))
             for i in range(lanes):
-                value = left[s, i] + product(outer.get(s, i), green.get(i))
+                value = left[s, i] + product(outer.get(s, i), green.get(i), alone)
                 green.put((i,), value)
                 emit(s, i, value)
 
@@ -236,34 +244,37 @@
     in_turns(total, lanes, turn)
 
 
-def prepared(stage, coupling, coupling_t, segs):
-    def prepare(s):
-        value = stage[s]
-        coupling.put((s,), value)
-        coupling_t.put((s,), value.T)
-
-    over(1, segs, prepare)
+def by_distance(own, received, seg, segs):
+    for d in range(segs):
+        yield lax.rem(seg - d + segs, segs), own if d == 0 else received[d - 1][0]
+
+
+def prepared(own, received, coupling, coupling_t, seg, segs):
+    for s, block in by_distance(own, received, seg, segs):
+
+        @pl.when(s > 0)
+        def _():
+            value = block[...]
+            coupling.put((s,), value)
+            coupling_t.put((s,), value.T)
 
 
 def first_round(segs, count, lanes, index, levels, *refs):
     own_matrix, received_matrix, refs = taken(refs, segs, 2)
     own_coupling, received_coupling, refs = taken(refs, segs, 1)
-    first, combined, onsite, coupling, coupling_t, stage, left, left_pair, green, right, outer, power, poly, row_scale, sems, chosen, firsts = refs
+    first, combined, onsite, coupling, coupling_t, left, left_pair, green, right, outer, power, poly, row_scale, sems, chosen = refs
     at = (index[1], segs, lax.rem(index[0], 2))
-    copies = started(pieces(stage, own_coupling, received_coupling, at), sems.at[0])
-    copies += started([(first, firsts)], sems.at[2])
-    later = started(pieces(onsite, own_matrix, received_matrix, at), sems.at[1])
+    copies = started(pieces(onsite, own_matrix, received_matrix, at), sems)
     total = choose(index, levels, chosen, count)
     combined[...] = jnp.zeros_like(combined)
+    coupling, coupling_t = Pair(coupling), Pair(coupling_t)
+    prepared(own_coupling, received_coupling, coupling, coupling_t, index[1], segs)
     wait(copies)
-    coupling, coupling_t = Pair(coupling), Pair(coupling_t)
-    prepared(stage, coupling, coupling_t, segs)
-    wait(later)
     n = onsite.shape[1]
 
     def turn(at, width):
         for i in range(width):
-            left[0, i] = firsts[at + i]
+            left[0, i] = first[at + i]
 
         def matrix(s, i):
             return onsite[s] + jnp.where(eye_mask(n), chosen[at + i], 0.0)
@@ -283,38 +294,34 @@
     own_matrix, received_matrix, refs = taken(refs, segs, 2)
     own_coupling, received_coupling, refs = taken(refs, segs, 1)
     own_phonon, received_phonon, refs = taken(refs, segs, 1)
-    combined_in, green_out, energy_out, *refs = refs
-    onsite, coupling, coupling_t, stage, left, left_pair, green, right, outer, power, poly, row_scale, sems, phonon, combined = refs
+    combined, green_out, energy_out, *refs = refs
+    onsite, coupling, coupling_t, left, left_pair, green, right, outer, power, poly, row_scale, sems, scattered = refs
     seg = index[1]
-    at = (seg, segs, lax.rem(index[0], 2))
-    copies = started([(combined_in, combined)], sems.at[3])
-    copies += started(pieces(phonon, own_phonon, received_phonon, at), sems.at[2])
-    later = started(pieces(onsite, own_matrix, received_matrix, at), sems.at[0])
-    later += started(pieces(stage, own_coupling, received_coupling, at), sems.at[1])
+    copies = started(pieces(onsite, own_matrix, received_matrix, (seg, segs, lax.rem(index[0], 2))), sems)
     coupling, coupling_t, right, outer = Pair(coupling), Pair(coupling_t), Pair(right), Pair(outer)
     n = onsite.shape[1]
+    blocks = list(by_distance(own_phonon, received_phonon, seg, segs))
+    for d, (s, block) in enumerate(blocks):
+        coupling.put((d,), block[...])
+        right.put((d, 0), combined[s])
+        outer.put((d, 0), product(coupling.get(d), right.get(d, 0)))
+        coupling_t.put((d,), block[...].T)
+    for d, (s, block) in enumerate(blocks):
+        value = product(outer.get(d, 0), coupling_t.get(d), True)
+        scattered[s] = value
+        if d == 0:
+            energy_out[...] = value
+    prepared(own_coupling, received_coupling, coupling, coupling_t, seg, segs)
     wait(copies)
-    for s in range(segs):
-        value = phonon[s]
-        coupling.put((s,), value)
-        coupling_t.put((s,), value.T)
-        right.put((s, 0), combined[s])
-    for s in range(segs):
-        outer.put((s, 0), product(coupling.get(s), right.get(s, 0)))
-    for s in range(segs):
-        combined[s] = product(outer.get(s, 0), coupling_t.get(s))
-    energy_out[...] = combined[seg]
-    wait(later)
 
     def matrix(s, i):
-        return onsite[s] + jnp.where(eye_mask(n), level[0], 0.0) + combined[s]
+        return onsite[s] + jnp.where(eye_mask(n), level[0], 0.0) + scattered[s]
 
     def emit(s, i, value):
         @pl.when(seg == s)
         def _():
             green_out[...] = value
 
-    prepared(stage, coupling, coupling_t, segs)
     sweep(
         1, segs, matrix, coupling, coupling_t, left, Pair(left_pair), Pair(green),
         (right, outer), Pair(power), Pair(poly), row_scale, emit, lambda s: seg <= s,
@@ -331,9 +338,9 @@
 
 def workspace(segs, n, lanes):
     return [
-        full(n, segs), pair(n, segs), pair(n, segs), full(n, segs), full(n, segs, lanes), pair(n, lanes), pair(n, lanes),
+        full(n, segs), pair(n, segs), pair(n, segs), full(n, segs, lanes), pair(n, lanes), pair(n, lanes),
         pair(n, segs, lanes), pair(n, segs, lanes), pair(n, lanes), pair(n, lanes), pltpu.VMEM((lanes, n, 128), F32),
-        pltpu.SemaphoreType.DMA((4, 2 * segs)),
+        pltpu.SemaphoreType.DMA((2 * segs,)),
     ]
 
 
@@ -341,16 +348,16 @@
     return sum(4 * math.prod(s.shape) for s in shapes if s.dtype == F32) + sum(2 * math.prod(s.shape) for s in shapes if s.dtype == BF16)
 
 
-def call(body, out_shape, operands, scratch, flops):
+def call(body, out_shape, operands, scratch, flops, copied):
     smem, vmem, anywhere = (pl.BlockSpec(memory_space=m) for m in (pltpu.SMEM, pltpu.VMEM, pl.ANY))
     outs = jax.tree.leaves(out_shape)
     return pl.pallas_call(
         body,
         out_shape=out_shape,
-        in_specs=[smem, smem] + [anywhere] * (len(operands) - 2),
+        in_specs=[smem, smem] + [anywhere] * copied + [vmem] * (len(operands) - 2 - copied),
         out_specs=jax.tree.map(lambda _: vmem, out_shape),
         scratch_shapes=scratch,
-        compiler_params=pltpu.CompilerParams(vmem_limit_bytes=held(scratch + outs) + SPARE_BYTES),
+        compiler_params=pltpu.CompilerParams(vmem_limit_bytes=held(scratch + outs + list(operands[2 + copied :])) + SPARE_BYTES),
         cost_estimate=pl.CostEstimate(flops=flops, bytes_accessed=held(outs), transcendentals=0),
     )(*operands)
 
@@ -413,7 +420,7 @@
     couplings = from_others(coupling)
     phonons = from_others(phonon)
     index = jnp.concatenate([jnp.stack([energy, seg]).astype(jnp.int32), offsets])
-    lanes = 2 if held(workspace(segs, n, 2)) + segs * 4 * n * n < VMEM_BYTES else 1
+    lanes = 2 if held(workspace(segs, n, 2)) + (2 * segs + TERMS) * 4 * n * n < VMEM_BYTES else 1
     shape = functools.partial(jax.ShapeDtypeStruct, dtype=F32)
     chosen = pltpu.SMEM((2 * TERMS,), jnp.float32)
     first = call(
@@ -422,20 +429,23 @@
         [index, all_levels, matrix, *matrices],
         [full(n), pair(n, lanes), pair(n, lanes), pltpu.VMEM((lanes, n, 128), F32), pltpu.SemaphoreType.DMA((2,)), chosen],
         12 * n**3 * TERMS * 3,
+        2 * segs - 1,
     )
     combined = call(
         functools.partial(first_round, segs, count, lanes),
         shape((segs, n, n)),
         [index, all_levels, matrix, *matrices, coupling, *couplings, first],
-        workspace(segs, n, lanes) + [chosen, full(n, TERMS)],
+        workspace(segs, n, lanes) + [chosen],
         22 * n**3 * TERMS * 3 * (segs - 1),
+        2 * segs - 1,
     )
     green, self_energy = call(
         functools.partial(second_round, segs),
         [shape((n, n))] * 2,
         [index, levels, matrix, *matrices, coupling, *couplings, phonon, *phonons, combined],
-        workspace(segs, n, 1) + [full(n, segs), full(n, segs)],
+        workspace(segs, n, 1) + [full(n, segs)],
         36 * n**3 * 3,
+        2 * segs - 1,
     )
     return green[None, None], self_energy[None, None]
 

time: 56.2 us -> 54 us (0.961)
  Pallas kernels: 32.8 us -> 30.7 us
    pallas_call x3, Pallas kernels: 32.8 us -> 30.7 us  [call(): pl.pallas_call(body, out_shape=out_shape, in_specs=[smem, smem] + [anywhe...]
where the time goes in v1:
time: 54 us; the launch traced here: 53.8 us
  Pallas kernels  30.7 us (57%)
  starting transfers between devices  10.8 us (20%)
  waiting for transfers between devices  5.95 us (11%)
  matrix products  3.85 us (7%)
  between operations  1.61 us (3%)
  other arithmetic  1 us (2%)
    pallas_call x3, Pallas kernels, call(): pl.pallas_call(body, out_shape=out_shape, in_specs=[smem, smem] + [anywhe...  30.7 us
    ppermute x5, starting transfers between devices, partner(): return lax.ppermute(block, axis, [(i, i ^ bit) for i in range(size)])  5.68 us
    ppermute x5, waiting for transfers between devices, partner(): return lax.ppermute(block, axis, [(i, i ^ bit) for i in range(size)])  5.21 us
    ppermute x3, starting transfers between devices, swapped(): lax.ppermute(block, axis, [(i, (i + distance) % size) for i in range(size)])  5.08 us
    dot_general x2, matrix products, less_lead(): lead = jnp.matmul(rows, coupling.T, precision=lax.Precision.HIGH) * 0.25  3.85 us
  transfers between devices with their start and end apart: 8, of which 4 were waited for; matrix products, arithmetic and copies ran while one was open for 6% of the time, Pallas kernels for 33%

profile of v1, /device:TPU:0, one launch (start us, length us, event | category | flops | bytes accessed | tf_op | source)
XLA Modules:
  0.0 53.8 jit_solution(10294840493567403866)
XLA Ops:
  0.6 0.0 copy-start.2
  0.7 1.7 %fusion.3 = f32[192,384]{1,0:T(8,128)S(1)} fusion(f32[1,384,384]{2,1,0:T(8,128)} %param.6, s32[]{:T(128)S(6)} %select_n.63, f32[1,384,384]{2,1,0:T(8,128)} %param.5, pred[]{:T(512)S(6)} %eq.19), kind=kOutput, calls=%fused_computation.5 | convolution fusion | flops 170090496 | bytes 1476096 | tf_op jit(solution)/shard_map/dot_general | solution.py:412
  2.4 3.1 %collective-permute-start = (f32[192,384]{1,0:T(8,128)S(1)}, f32[192,384]{1,0:T(8,128)S(1)}, u32[]{:S(2)}, u32[]{:S(2)}) collective-permute-start(f32[192,384]{1,0:T(8,128)S(1)} %fusion.3), channel_id=1, source_target_pairs={{0,1},{1,0},{2,3},{3,2},{4,5},{5,4},{6,7},{7,6},{8,9},{9,8},{10,11... | collective-permute-start | bytes 884744 | tf_op jit(solution)/shard_map/ppermute | solution.py:367
  5.4 0.0 collective-permute-start.4
  5.4 0.2 collective-permute-start.2
  5.6 1.9 %collective-permute-start.3 = (f32[384,384]{1,0:T(8,128)}, f32[384,384]{1,0:T(8,128)S(1)}, u32[]{:S(2)}, u32[]{:S(2)}) collective-permute-start(f32[384,384]{1,0:T(8,128)} %bitcast.22), channel_id=1, source_target_pairs={{0,1},{1,0},{2,3},{3,2},{4,5},{5,4},{6,7},{7,6},{8,9},{9,8},{10,11... | collective-permute-start | bytes 1769480 | tf_op jit(solution)/shard_map/ppermute | solution.py:367
  7.5 2.1 %fusion.1.refs_0_ = f32[384,384]{1,0:T(8,128)S(1)} fusion(f32[384,384]{1,0:T(8,128)} %bitcast.19, f32[1,384,384]{2,1,0:T(8,128)} %param.5, pred[]{:T(512)S(6)} %eq.19, f32[1,384,384]{2,1,0:T(8,128)} %param.6), kind=kOutput, calls=%fused_computation.2 | convolution fusion | flops 340180992 | bytes 2359297 | tf_op jit(solution)/shard_map/dot_general | solution.py:412
  10.3 0.0 copy-done.2
  10.3 0.1 pad_add_fusion.index
  10.4 0.0 collective-permute-done.4
  10.4 0.7 %broadcast_select_fusion = f32[2]{0:T(128)S(1)} fusion(pred[]{:T(512)S(6)} %eq.23, f32[1]{0:T(128)} %collective-permute-done.4, f32[1]{0:T(128)S(6)} %copy.7.level), kind=kLoop, calls=%fused_computation.8 | loop fusion | flops 6 | bytes 17 | tf_op jit(solution)/shard_map/jit(_where)/select_n | solution.py:381
  11.1 1.5 %collective-permute-start.5 = (f32[2]{0:T(128)S(1)}, f32[2]{0:T(128)S(1)}, u32[]{:S(2)}, u32[]{:S(2)}) collective-permute-start(f32[2]{0:T(128)S(1)} %broadcast_select_fusion), channel_id=1, source_target_pairs={{0,4},{2,6},{4,0},{6,2},{8,12},{10,14},{12,8},{14,10},{16,20},{18,... | collective-permute-start | bytes 32 | tf_op jit(solution)/shard_map/ppermute | solution.py:372
  12.6 0.7 %collective-permute-done.refs_1_ = f32[192,384]{1,0:T(8,128)S(1)} collective-permute-done((f32[192,384]{1,0:T(8,128)S(1)}, f32[192,384]{1,0:T(8,128)S(1)}, u32[]{:S(2)}, u32[]{:S(2)}) %collective-permute-start) | collective-permute-done | bytes 294944 | tf_op jit(solution)/shard_map/ppermute | solution.py:367
  13.3 0.0 collective-permute-start.1
  13.3 1.3 %collective-permute-done.5 = f32[2]{0:T(128)S(1)} collective-permute-done((f32[2]{0:T(128)S(1)}, f32[2]{0:T(128)S(1)}, u32[]{:S(2)}, u32[]{:S(2)}) %collective-permute-start.5) | collective-permute-done | bytes 40 | tf_op jit(solution)/shard_map/ppermute | solution.py:372
  14.6 0.1 broadcast_select_fusion.1
  14.7 1.6 %collective-permute-start.6 = (f32[4]{0:T(128)S(1)}, f32[4]{0:T(128)S(1)}, u32[]{:S(2)}, u32[]{:S(2)}) collective-permute-start(f32[4]{0:T(128)S(1)} %broadcast_select_fusion.1), channel_id=1, source_target_pairs={{0,8},{2,10},{4,12},{6,14},{8,0},{10,2},{12,4},{14,6},{16,24},{18,... | collective-permute-start | bytes 56 | tf_op jit(solution)/shard_map/ppermute | solution.py:372
  16.3 2.0 %collective-permute-done.6 = f32[4]{0:T(128)S(1)} collective-permute-done((f32[4]{0:T(128)S(1)}, f32[4]{0:T(128)S(1)}, u32[]{:S(2)}, u32[]{:S(2)}) %collective-permute-start.6) | collective-permute-done | bytes 48 | tf_op jit(solution)/shard_map/ppermute | solution.py:372
  18.3 0.1 broadcast_select_fusion.2
  18.4 2.6 %collective-permute-start.7 = (f32[8]{0:T(128)S(1)}, f32[8]{0:T(128)S(1)}, u32[]{:S(2)}, u32[]{:S(2)}) collective-permute-start(f32[8]{0:T(128)S(1)} %broadcast_select_fusion.2), channel_id=1, source_target_pairs={{0,16},{2,18},{4,20},{6,22},{8,24},{10,26},{12,28},{14,30},{16,0},... | collective-permute-start | bytes 104 | tf_op jit(solution)/shard_map/ppermute | solution.py:372
  21.0 1.9 %collective-permute-done.7 = f32[8]{0:T(128)S(1)} collective-permute-done((f32[8]{0:T(128)S(1)}, f32[8]{0:T(128)S(1)}, u32[]{:S(2)}, u32[]{:S(2)}) %collective-permute-start.7) | collective-permute-done | bytes 64 | tf_op jit(solution)/shard_map/ppermute | solution.py:372
  22.8 0.1 broadcast_select_fusion.3.levels
  22.9 0.0 copy-start
  22.9 0.0 collective-permute-done.1.refs_2_
  22.9 6.2 %shard_map.68.refs_5_ = f32[4,384,384]{2,1,0:T(8,128)S(1)} custom-call(s32[4]{0:T(128)S(1)} %pad_add_fusion.index, f32[16]{0:T(128)S(1)} %broadcast_select_fusion.3.levels, f32[384,384]{1,0:T(8,128)S(1)} %fusion.1.refs_0_, f32[192,384]{1,0:T(8,128)S(1)} %collective-permute-done.refs_1_, f32[192,384]{1,0:T(8,128)S(1)} %collective-permute-done.1.refs_2_), custom_call_target="tpu_custom_call" | custom-call | flops 8153726976 | bytes 2359296 | tf_op jit(solution)/shard_map/pallas_call | solution.py:354
  29.2 0.0 copy-start.1
  29.2 0.0 collective-permute-done.2.refs_4_
  29.2 0.0 copy-done
  29.2 11.7 %shard_map.69.refs_7_ = f32[2,384,384]{2,1,0:T(8,128)S(1)} custom-call(s32[4]{0:T(128)S(1)} %pad_add_fusion.index, f32[16]{0:T(128)S(1)} %broadcast_select_fusion.3.levels, f32[384,384]{1,0:T(8,128)S(1)} %fusion.1.refs_0_, f32[192,384]{1,0:T(8,128)S(1)} %collective-permute-done.refs_1_, f32[192,384]{1,0:T(8,128)S(1)} %collective-permute-done.1.refs_2_, ...), custom_call_target="tpu_custom_call" | custom-call | flops 14948499456 | bytes 1179648 | tf_op jit(solution)/shard_map/pallas_call | solution.py:354
  40.9 0.0 collective-permute-done.3.refs_6_
  40.9 0.0 copy-done.1
  40.9 12.7 %shard_map.70 = (f32[384,384]{1,0:T(8,128)}, f32[384,384]{1,0:T(8,128)}) custom-call(s32[4]{0:T(128)S(1)} %pad_add_fusion.index, f32[1]{0:T(128)S(6)} %copy.7.level, f32[384,384]{1,0:T(8,128)S(1)} %fusion.1.refs_0_, f32[192,384]{1,0:T(8,128)S(1)} %collective-permute-done.refs_1_, f32[192,384]{1,0:T(8,128)S(1)} %collective-permute-done.1.refs_2_, ...), custom_call_target="tpu_custom_call" | custom-call | flops 6115295232 | bytes 1179648 | tf_op jit(solution)/shard_map/pallas_call | solution.py:354
Async XLA Ops:
  0.6 9.6 %copy-start.2 = (s32[2]{0:T(128)S(1)}, s32[2]{0:T(128)}, u32[]{:S(2)}) copy-start(s32[2]{0:T(128)} %param.9) | copy-start | bytes 28
  2.4 10.9 %collective-permute-start = (f32[192,384]{1,0:T(8,128)S(1)}, f32[192,384]{1,0:T(8,128)S(1)}, u32[]{:S(2)}, u32[]{:S(2)}) collective-permute-start(f32[192,384]{1,0:T(8,128)S(1)} %fusion.3), channel_id=1, source_target_pairs={{0,1},{1,0},{2,3},{3,2},{4,5},{5,4},{6,7},{7,6},{8,9},{9,8},{10,11... | collective-permute-start | bytes 884744 | tf_op jit(solution)/shard_map/ppermute | solution.py:367
  5.4 4.9 %collective-permute-start.4 = (f32[1]{0:T(128)}, f32[1]{0:T(128)}, u32[]{:S(2)}, u32[]{:S(2)}) collective-permute-start(f32[1]{0:T(128)} %param.8), channel_id=1, source_target_pairs={{0,2},{2,0},{4,6},{6,4},{8,10},{10,8},{12,14},{14,12},{16,18},{18,... | collective-permute-start | bytes 20 | tf_op jit(solution)/shard_map/ppermute | solution.py:372
  5.4 23.7 %collective-permute-start.2 = (f32[384,384]{1,0:T(8,128)}, f32[384,384]{1,0:T(8,128)S(1)}, u32[]{:S(2)}, u32[]{:S(2)}) collective-permute-start(f32[384,384]{1,0:T(8,128)} %bitcast.18), channel_id=1, source_target_pairs={{0,1},{1,0},{2,3},{3,2},{4,5},{5,4},{6,7},{7,6},{8,9},{9,8},{10,11... | collective-permute-start | bytes 1769480 | tf_op jit(solution)/shard_map/ppermute | solution.py:367
  5.6 35.3 %collective-permute-start.3 = (f32[384,384]{1,0:T(8,128)}, f32[384,384]{1,0:T(8,128)S(1)}, u32[]{:S(2)}, u32[]{:S(2)}) collective-permute-start(f32[384,384]{1,0:T(8,128)} %bitcast.22), channel_id=1, source_target_pairs={{0,1},{1,0},{2,3},{3,2},{4,5},{5,4},{6,7},{7,6},{8,9},{9,8},{10,11... | collective-permute-start | bytes 1769480 | tf_op jit(solution)/shard_map/ppermute | solution.py:367
  11.1 3.6 %collective-permute-start.5 = (f32[2]{0:T(128)S(1)}, f32[2]{0:T(128)S(1)}, u32[]{:S(2)}, u32[]{:S(2)}) collective-permute-start(f32[2]{0:T(128)S(1)} %broadcast_select_fusion), channel_id=1, source_target_pairs={{0,4},{2,6},{4,0},{6,2},{8,12},{10,14},{12,8},{14,10},{16,20},{18,... | collective-permute-start | bytes 32 | tf_op jit(solution)/shard_map/ppermute | solution.py:372
  13.3 9.6 %collective-permute-start.1 = (f32[192,384]{1,0:T(8,128)S(1)}, f32[192,384]{1,0:T(8,128)S(1)}, u32[]{:S(2)}, u32[]{:S(2)}) collective-permute-start(f32[192,384]{1,0:T(8,128)S(1)} %collective-permute-done.refs_1_), channel_id=1, source_target_pairs={{0,2},{2,0},{4,6},{6,4},{8,10},{10,8},{12,14},{14,12},{16,18},{18,... | collective-permute-start | bytes 884744 | tf_op jit(solution)/shard_map/ppermute | solution.py:372
  14.7 3.6 %collective-permute-start.6 = (f32[4]{0:T(128)S(1)}, f32[4]{0:T(128)S(1)}, u32[]{:S(2)}, u32[]{:S(2)}) collective-permute-start(f32[4]{0:T(128)S(1)} %broadcast_select_fusion.1), channel_id=1, source_target_pairs={{0,8},{2,10},{4,12},{6,14},{8,0},{10,2},{12,4},{14,6},{16,24},{18,... | collective-permute-start | bytes 56 | tf_op jit(solution)/shard_map/ppermute | solution.py:372
  18.4 4.5 %collective-permute-start.7 = (f32[8]{0:T(128)S(1)}, f32[8]{0:T(128)S(1)}, u32[]{:S(2)}, u32[]{:S(2)}) collective-permute-start(f32[8]{0:T(128)S(1)} %broadcast_select_fusion.2), channel_id=1, source_target_pairs={{0,16},{2,18},{4,20},{6,22},{8,24},{10,26},{12,28},{14,30},{16,0},... | collective-permute-start | bytes 104 | tf_op jit(solution)/shard_map/ppermute | solution.py:372
  22.9 6.3 %copy-start = (f32[1,384,384]{2,1,0:T(8,128)S(1)}, f32[1,384,384]{2,1,0:T(8,128)}, u32[]{:S(2)}) copy-start(f32[1,384,384]{2,1,0:T(8,128)} %param.6) | copy-start | bytes 1769476
  29.2 11.8 %copy-start.1 = (f32[1,384,384]{2,1,0:T(8,128)S(1)}, f32[1,384,384]{2,1,0:T(8,128)}, u32[]{:S(2)}) copy-start(f32[1,384,384]{2,1,0:T(8,128)} %param.7) | copy-start | bytes 1769476

commit v2 on v1

--- a/solution.py
+++ b/solution.py
@@ -251,12 +251,9 @@
 
 def prepared(own, received, coupling, coupling_t, seg, segs):
     for s, block in by_distance(own, received, seg, segs):
-
-        @pl.when(s > 0)
-        def _():
-            value = block[...]
-            coupling.put((s,), value)
-            coupling_t.put((s,), value.T)
+        value = block[...]
+        coupling.put((s,), value)
+        coupling_t.put((s,), value.T)
 
 
 def first_round(segs, count, lanes, index, levels, *refs):
@@ -295,24 +292,25 @@
     own_coupling, received_coupling, refs = taken(refs, segs, 1)
     own_phonon, received_phonon, refs = taken(refs, segs, 1)
     combined, green_out, energy_out, *refs = refs
-    onsite, coupling, coupling_t, left, left_pair, green, right, outer, power, poly, row_scale, sems, scattered = refs
+    onsite, coupling, coupling_t, left, left_pair, green, right, outer, power, poly, row_scale, sems, scattered, phonon, phonon_t = refs
     seg = index[1]
     copies = started(pieces(onsite, own_matrix, received_matrix, (seg, segs, lax.rem(index[0], 2))), sems)
     coupling, coupling_t, right, outer = Pair(coupling), Pair(coupling_t), Pair(right), Pair(outer)
+    phonon, phonon_t = Pair(phonon), Pair(phonon_t)
     n = onsite.shape[1]
     blocks = list(by_distance(own_phonon, received_phonon, seg, segs))
     for d, (s, block) in enumerate(blocks):
-        coupling.put((d,), block[...])
+        phonon.put((d,), block[...])
         right.put((d, 0), combined[s])
-        outer.put((d, 0), product(coupling.get(d), right.get(d, 0)))
-        coupling_t.put((d,), block[...].T)
+        outer.put((d, 0), product(phonon.get(d), right.get(d, 0)))
+        phonon_t.put((d,), block[...].T)
+    prepared(own_coupling, received_coupling, coupling, coupling_t, seg, segs)
+    wait(copies)
     for d, (s, block) in enumerate(blocks):
-        value = product(outer.get(d, 0), coupling_t.get(d), True)
+        value = product(outer.get(d, 0), phonon_t.get(d), True)
         scattered[s] = value
         if d == 0:
             energy_out[...] = value
-    prepared(own_coupling, received_coupling, coupling, coupling_t, seg, segs)
-    wait(copies)
 
     def matrix(s, i):
         return onsite[s] + jnp.where(eye_mask(n), level[0], 0.0) + scattered[s]
@@ -443,7 +441,7 @@
         functools.partial(second_round, segs),
         [shape((n, n))] * 2,
         [index, levels, matrix, *matrices, coupling, *couplings, phonon, *phonons, combined],
-        workspace(segs, n, 1) + [full(n, segs)],
+        workspace(segs, n, 1) + [full(n, segs), pair(n, segs), pair(n, segs)],
         36 * n**3 * 3,
         2 * segs - 1,
     )

time: 54 us -> 54.1 us (level)
  transfers between devices with their start and end apart: 8 -> 8, of which waited for: 4 -> 4; matrix products, arithmetic and copies ran while one was open for 6% -> 6% of each run, Pallas kernels for 33% -> 34%
where the time goes in v2:
time: 54.1 us; the launch traced here: 53.9 us
  Pallas kernels  30.7 us (57%)
  starting transfers between devices  10.8 us (20%)
  waiting for transfers between devices  5.95 us (11%)
  matrix products  3.85 us (7%)
  between operations  1.59 us (3%)
  other arithmetic  1 us (2%)
    pallas_call x3, Pallas kernels, call(): pl.pallas_call(body, out_shape=out_shape, in_specs=[smem, smem] + [anywhe...  30.7 us
    ppermute x5, starting transfers between devices, partner(): return lax.ppermute(block, axis, [(i, i ^ bit) for i in range(size)])  5.68 us
    ppermute x5, waiting for transfers between devices, partner(): return lax.ppermute(block, axis, [(i, i ^ bit) for i in range(size)])  5.21 us
    ppermute x3, starting transfers between devices, swapped(): lax.ppermute(block, axis, [(i, (i + distance) % size) for i in range(size)])  5.08 us
    dot_general x2, matrix products, less_lead(): lead = jnp.matmul(rows, coupling.T, precision=lax.Precision.HIGH) * 0.25  3.85 us
  transfers between devices with their start and end apart: 8, of which 4 were waited for; matrix products, arithmetic and copies ran while one was open for 6% of the time, Pallas kernels for 34%

profile of v2, /device:TPU:0, one launch (start us, length us, event | category | flops | bytes accessed | tf_op | source)
XLA Modules:
  0.0 53.9 jit_solution(3795271585199690422)
XLA Ops:
  0.6 0.0 copy-start.2
  0.7 1.7 %fusion.3 = f32[192,384]{1,0:T(8,128)S(1)} fusion(f32[1,384,384]{2,1,0:T(8,128)} %param.6, s32[]{:T(128)S(6)} %select_n.63, f32[1,384,384]{2,1,0:T(8,128)} %param.5, pred[]{:T(512)S(6)} %eq.19), kind=kOutput, calls=%fused_computation.5 | convolution fusion | flops 170090496 | bytes 1476096 | tf_op jit(solution)/shard_map/dot_general | solution.py:410
  2.4 3.1 %collective-permute-start = (f32[192,384]{1,0:T(8,128)S(1)}, f32[192,384]{1,0:T(8,128)S(1)}, u32[]{:S(2)}, u32[]{:S(2)}) collective-permute-start(f32[192,384]{1,0:T(8,128)S(1)} %fusion.3), channel_id=1, source_target_pairs={{0,1},{1,0},{2,3},{3,2},{4,5},{5,4},{6,7},{7,6},{8,9},{9,8},{10,11... | collective-permute-start | bytes 884744 | tf_op jit(solution)/shard_map/ppermute | solution.py:365
  5.4 0.0 collective-permute-start.4
  5.4 0.2 collective-permute-start.2
  5.6 1.9 %collective-permute-start.3 = (f32[384,384]{1,0:T(8,128)}, f32[384,384]{1,0:T(8,128)S(1)}, u32[]{:S(2)}, u32[]{:S(2)}) collective-permute-start(f32[384,384]{1,0:T(8,128)} %bitcast.22), channel_id=1, source_target_pairs={{0,1},{1,0},{2,3},{3,2},{4,5},{5,4},{6,7},{7,6},{8,9},{9,8},{10,11... | collective-permute-start | bytes 1769480 | tf_op jit(solution)/shard_map/ppermute | solution.py:365
  7.5 2.1 %fusion.1.refs_0_ = f32[384,384]{1,0:T(8,128)S(1)} fusion(f32[384,384]{1,0:T(8,128)} %bitcast.19, f32[1,384,384]{2,1,0:T(8,128)} %param.5, pred[]{:T(512)S(6)} %eq.19, f32[1,384,384]{2,1,0:T(8,128)} %param.6), kind=kOutput, calls=%fused_computation.2 | convolution fusion | flops 340180992 | bytes 2359297 | tf_op jit(solution)/shard_map/dot_general | solution.py:410
  10.3 0.0 copy-done.2
  10.3 0.1 pad_add_fusion.index
  10.4 0.0 collective-permute-done.4
  10.4 0.7 %broadcast_select_fusion = f32[2]{0:T(128)S(1)} fusion(pred[]{:T(512)S(6)} %eq.23, f32[1]{0:T(128)} %collective-permute-done.4, f32[1]{0:T(128)S(6)} %copy.7.level), kind=kLoop, calls=%fused_computation.8 | loop fusion | flops 6 | bytes 17 | tf_op jit(solution)/shard_map/jit(_where)/select_n | solution.py:379
  11.1 1.5 %collective-permute-start.5 = (f32[2]{0:T(128)S(1)}, f32[2]{0:T(128)S(1)}, u32[]{:S(2)}, u32[]{:S(2)}) collective-permute-start(f32[2]{0:T(128)S(1)} %broadcast_select_fusion), channel_id=1, source_target_pairs={{0,4},{2,6},{4,0},{6,2},{8,12},{10,14},{12,8},{14,10},{16,20},{18,... | collective-permute-start | bytes 32 | tf_op jit(solution)/shard_map/ppermute | solution.py:370
  12.6 0.7 %collective-permute-done.refs_1_ = f32[192,384]{1,0:T(8,128)S(1)} collective-permute-done((f32[192,384]{1,0:T(8,128)S(1)}, f32[192,384]{1,0:T(8,128)S(1)}, u32[]{:S(2)}, u32[]{:S(2)}) %collective-permute-start) | collective-permute-done | bytes 294944 | tf_op jit(solution)/shard_map/ppermute | solution.py:365
  13.3 0.0 collective-permute-start.1
  13.3 1.3 %collective-permute-done.5 = f32[2]{0:T(128)S(1)} collective-permute-done((f32[2]{0:T(128)S(1)}, f32[2]{0:T(128)S(1)}, u32[]{:S(2)}, u32[]{:S(2)}) %collective-permute-start.5) | collective-permute-done | bytes 40 | tf_op jit(solution)/shard_map/ppermute | solution.py:370
  14.6 0.1 broadcast_select_fusion.1
  14.7 1.6 %collective-permute-start.6 = (f32[4]{0:T(128)S(1)}, f32[4]{0:T(128)S(1)}, u32[]{:S(2)}, u32[]{:S(2)}) collective-permute-start(f32[4]{0:T(128)S(1)} %broadcast_select_fusion.1), channel_id=1, source_target_pairs={{0,8},{2,10},{4,12},{6,14},{8,0},{10,2},{12,4},{14,6},{16,24},{18,... | collective-permute-start | bytes 56 | tf_op jit(solution)/shard_map/ppermute | solution.py:370
  16.3 2.0 %collective-permute-done.6 = f32[4]{0:T(128)S(1)} collective-permute-done((f32[4]{0:T(128)S(1)}, f32[4]{0:T(128)S(1)}, u32[]{:S(2)}, u32[]{:S(2)}) %collective-permute-start.6) | collective-permute-done | bytes 48 | tf_op jit(solution)/shard_map/ppermute | solution.py:370
  18.3 0.1 broadcast_select_fusion.2
  18.4 2.6 %collective-permute-start.7 = (f32[8]{0:T(128)S(1)}, f32[8]{0:T(128)S(1)}, u32[]{:S(2)}, u32[]{:S(2)}) collective-permute-start(f32[8]{0:T(128)S(1)} %broadcast_select_fusion.2), channel_id=1, source_target_pairs={{0,16},{2,18},{4,20},{6,22},{8,24},{10,26},{12,28},{14,30},{16,0},... | collective-permute-start | bytes 104 | tf_op jit(solution)/shard_map/ppermute | solution.py:370
  21.0 1.9 %collective-permute-done.7 = f32[8]{0:T(128)S(1)} collective-permute-done((f32[8]{0:T(128)S(1)}, f32[8]{0:T(128)S(1)}, u32[]{:S(2)}, u32[]{:S(2)}) %collective-permute-start.7) | collective-permute-done | bytes 64 | tf_op jit(solution)/shard_map/ppermute | solution.py:370
  22.8 0.1 broadcast_select_fusion.3.levels
  22.9 0.0 copy-start
  22.9 0.0 collective-permute-done.1.refs_2_
  22.9 6.2 %shard_map.68.refs_5_ = f32[4,384,384]{2,1,0:T(8,128)S(1)} custom-call(s32[4]{0:T(128)S(1)} %pad_add_fusion.index, f32[16]{0:T(128)S(1)} %broadcast_select_fusion.3.levels, f32[384,384]{1,0:T(8,128)S(1)} %fusion.1.refs_0_, f32[192,384]{1,0:T(8,128)S(1)} %collective-permute-done.refs_1_, f32[192,384]{1,0:T(8,128)S(1)} %collective-permute-done.1.refs_2_), custom_call_target="tpu_custom_call" | custom-call | flops 8153726976 | bytes 2359296 | tf_op jit(solution)/shard_map/pallas_call | solution.py:352
  29.2 0.0 copy-start.1
  29.2 0.0 collective-permute-done.2.refs_4_
  29.2 0.0 copy-done
  29.2 11.8 %shard_map.69.refs_7_ = f32[2,384,384]{2,1,0:T(8,128)S(1)} custom-call(s32[4]{0:T(128)S(1)} %pad_add_fusion.index, f32[16]{0:T(128)S(1)} %broadcast_select_fusion.3.levels, f32[384,384]{1,0:T(8,128)S(1)} %fusion.1.refs_0_, f32[192,384]{1,0:T(8,128)S(1)} %collective-permute-done.refs_1_, f32[192,384]{1,0:T(8,128)S(1)} %collective-permute-done.1.refs_2_, ...), custom_call_target="tpu_custom_call" | custom-call | flops 14948499456 | bytes 1179648 | tf_op jit(solution)/shard_map/pallas_call | solution.py:352
  41.0 0.0 collective-permute-done.3.refs_6_
  41.1 0.0 copy-done.1
  41.1 12.6 %shard_map.70 = (f32[384,384]{1,0:T(8,128)}, f32[384,384]{1,0:T(8,128)}) custom-call(s32[4]{0:T(128)S(1)} %pad_add_fusion.index, f32[1]{0:T(128)S(6)} %copy.7.level, f32[384,384]{1,0:T(8,128)S(1)} %fusion.1.refs_0_, f32[192,384]{1,0:T(8,128)S(1)} %collective-permute-done.refs_1_, f32[192,384]{1,0:T(8,128)S(1)} %collective-permute-done.1.refs_2_, ...), custom_call_target="tpu_custom_call" | custom-call | flops 6115295232 | bytes 1179648 | tf_op jit(solution)/shard_map/pallas_call | solution.py:352
Async XLA Ops:
  0.6 9.6 %copy-start.2 = (s32[2]{0:T(128)S(1)}, s32[2]{0:T(128)}, u32[]{:S(2)}) copy-start(s32[2]{0:T(128)} %param.9) | copy-start | bytes 28
  2.4 10.9 %collective-permute-start = (f32[192,384]{1,0:T(8,128)S(1)}, f32[192,384]{1,0:T(8,128)S(1)}, u32[]{:S(2)}, u32[]{:S(2)}) collective-permute-start(f32[192,384]{1,0:T(8,128)S(1)} %fusion.3), channel_id=1, source_target_pairs={{0,1},{1,0},{2,3},{3,2},{4,5},{5,4},{6,7},{7,6},{8,9},{9,8},{10,11... | collective-permute-start | bytes 884744 | tf_op jit(solution)/shard_map/ppermute | solution.py:365
  5.4 4.9 %collective-permute-start.4 = (f32[1]{0:T(128)}, f32[1]{0:T(128)}, u32[]{:S(2)}, u32[]{:S(2)}) collective-permute-start(f32[1]{0:T(128)} %param.8), channel_id=1, source_target_pairs={{0,2},{2,0},{4,6},{6,4},{8,10},{10,8},{12,14},{14,12},{16,18},{18,... | collective-permute-start | bytes 20 | tf_op jit(solution)/shard_map/ppermute | solution.py:370
  5.4 23.7 %collective-permute-start.2 = (f32[384,384]{1,0:T(8,128)}, f32[384,384]{1,0:T(8,128)S(1)}, u32[]{:S(2)}, u32[]{:S(2)}) collective-permute-start(f32[384,384]{1,0:T(8,128)} %bitcast.18), channel_id=1, source_target_pairs={{0,1},{1,0},{2,3},{3,2},{4,5},{5,4},{6,7},{7,6},{8,9},{9,8},{10,11... | collective-permute-start | bytes 1769480 | tf_op jit(solution)/shard_map/ppermute | solution.py:365
  5.6 35.4 %collective-permute-start.3 = (f32[384,384]{1,0:T(8,128)}, f32[384,384]{1,0:T(8,128)S(1)}, u32[]{:S(2)}, u32[]{:S(2)}) collective-permute-start(f32[384,384]{1,0:T(8,128)} %bitcast.22), channel_id=1, source_target_pairs={{0,1},{1,0},{2,3},{3,2},{4,5},{5,4},{6,7},{7,6},{8,9},{9,8},{10,11... | collective-permute-start | bytes 1769480 | tf_op jit(solution)/shard_map/ppermute | solution.py:365
  11.1 3.6 %collective-permute-start.5 = (f32[2]{0:T(128)S(1)}, f32[2]{0:T(128)S(1)}, u32[]{:S(2)}, u32[]{:S(2)}) collective-permute-start(f32[2]{0:T(128)S(1)} %broadcast_select_fusion), channel_id=1, source_target_pairs={{0,4},{2,6},{4,0},{6,2},{8,12},{10,14},{12,8},{14,10},{16,20},{18,... | collective-permute-start | bytes 32 | tf_op jit(solution)/shard_map/ppermute | solution.py:370
  13.3 9.6 %collective-permute-start.1 = (f32[192,384]{1,0:T(8,128)S(1)}, f32[192,384]{1,0:T(8,128)S(1)}, u32[]{:S(2)}, u32[]{:S(2)}) collective-permute-start(f32[192,384]{1,0:T(8,128)S(1)} %collective-permute-done.refs_1_), channel_id=1, source_target_pairs={{0,2},{2,0},{4,6},{6,4},{8,10},{10,8},{12,14},{14,12},{16,18},{18,... | collective-permute-start | bytes 884744 | tf_op jit(solution)/shard_map/ppermute | solution.py:370
  14.7 3.6 %collective-permute-start.6 = (f32[4]{0:T(128)S(1)}, f32[4]{0:T(128)S(1)}, u32[]{:S(2)}, u32[]{:S(2)}) collective-permute-start(f32[4]{0:T(128)S(1)} %broadcast_select_fusion.1), channel_id=1, source_target_pairs={{0,8},{2,10},{4,12},{6,14},{8,0},{10,2},{12,4},{14,6},{16,24},{18,... | collective-permute-start | bytes 56 | tf_op jit(solution)/shard_map/ppermute | solution.py:370
  18.4 4.5 %collective-permute-start.7 = (f32[8]{0:T(128)S(1)}, f32[8]{0:T(128)S(1)}, u32[]{:S(2)}, u32[]{:S(2)}) collective-permute-start(f32[8]{0:T(128)S(1)} %broadcast_select_fusion.2), channel_id=1, source_target_pairs={{0,16},{2,18},{4,20},{6,22},{8,24},{10,26},{12,28},{14,30},{16,0},... | collective-permute-start | bytes 104 | tf_op jit(solution)/shard_map/ppermute | solution.py:370
  22.9 6.3 %copy-start = (f32[1,384,384]{2,1,0:T(8,128)S(1)}, f32[1,384,384]{2,1,0:T(8,128)}, u32[]{:S(2)}) copy-start(f32[1,384,384]{2,1,0:T(8,128)} %param.6) | copy-start | bytes 1769476
  29.2 11.9 %copy-start.1 = (f32[1,384,384]{2,1,0:T(8,128)S(1)}, f32[1,384,384]{2,1,0:T(8,128)}, u32[]{:S(2)}) copy-start(f32[1,384,384]{2,1,0:T(8,128)} %param.7) | copy-start | bytes 1769476
